TPU v7x, 32 devices: a whole 2x2x4 slice. The times are simulated.
32 devices in a mesh: gx: 8 (over y, x, core), gy: 4 (over z).
Axes of the slice: x: 2, y: 2, z: 4, core: 2. Of those that a mesh axis runs over, the one named last changes fastest.
Arguments:
- coefficients: float32 [2, 2048, 512], P(None, 'gx', 'gy'), may hold values from -0.125 to 0.125
- spacing: float32 [31], replicated, may hold values from 0.6 to 1.5
Outputs:
- zcoord: float32 [32, 4096, 512], P(None, 'gx', 'gy')
- slopes: float32 [2, 32, 4096, 512], P(None, None, 'gx', 'gy')
- jacobian: float32 [32, 4096, 512], P(None, 'gx', 'gy')
- quality: float32 [32, 4096, 512], P(None, 'gx', 'gy')
All inputs are finite; a program needn't handle non-finite values.
Results may differ from a plain program's by a relative error of at most 0.0003.
Values sent between devices are 32-bit elements; how exact they have to be, the bound alone decides.
A program may use at most 128 MiB of HBM per device.

v0:
```python
import functools
import math

import jax
import jax.numpy as jnp
import numpy as np
from jax import lax
from jax.experimental import pallas as pl
from jax.experimental.pallas import tpu as pltpu
from jax.sharding import PartitionSpec as P

NX = 4096


BOUNDARY = (
    (-24.0 / 17.0, 59.0 / 34.0, -4.0 / 17.0, -3.0 / 34.0, 0.0, 0.0),
    (-0.5, 0.0, 0.5, 0.0, 0.0, 0.0),
    (4.0 / 43.0, -59.0 / 86.0, 0.0, 59.0 / 86.0, -4.0 / 43.0, 0.0),
    (3.0 / 98.0, 0.0, -59.0 / 98.0, 0.0, 32.0 / 49.0, -4.0 / 49.0),
)
TOPO_SCALE = 0.1


def extended(cells, sides, width):
    for axis, dim in sides:
        count = lax.axis_size(axis)
        head = lax.slice_in_dim(cells, 0, width, axis=dim)
        tail = lax.slice_in_dim(cells, cells.shape[dim] - width, cells.shape[dim], axis=dim)
        cells = jnp.concatenate(
            [
                lax.ppermute(tail, axis, [(i, (i + 1) % count) for i in range(count)]),
                cells,
                lax.ppermute(head, axis, [((i + 1) % count, i) for i in range(count)]),
            ],
            axis=dim,
        )
    return cells


def vertical(field):
    levels = field.shape[0]
    top_rows = []
    bottom_rows = []
    for row_id in range(4):
        upper = None
        lower = None
        for level_id, factor in enumerate(BOUNDARY[row_id]):
            if factor != 0.0:
                term_up = factor * field[level_id]
                term_down = -factor * field[levels - 1 - level_id]
                upper = term_up if upper is None else upper + term_up
                lower = term_down if lower is None else lower + term_down
        top_rows.append(upper)
        bottom_rows.append(lower)
    inner = (
        8.0 * (field[5 : levels - 3] - field[3 : levels - 5])
        - (field[6 : levels - 2] - field[2 : levels - 6])
    ) / 12.0
    return jnp.concatenate([jnp.stack(top_rows), inner, jnp.stack(bottom_rows[::-1])], axis=0)


def stretching(spacing):
    summed = jnp.sum(spacing)
    return jnp.concatenate([jnp.zeros((1,), spacing.dtype), jnp.cumsum(spacing)]) / summed


def column_depth(surface, stretch):
    levels = stretch.shape[0]
    return (levels - 1.0) * (surface[None] + (1.0 - surface[None]) * stretch[:, None, None])


def basis(count, x_cells):
    mode_ids = jnp.arange(count, dtype=jnp.int32)
    phase = (mode_ids[:, None] * x_cells[None, :] % NX).astype(jnp.float32) * (2.0 * math.pi / NX)
    return (jnp.cos(phase), jnp.sin(phase))


def project(cosine, sine, portion):
    first = jnp.dot(
        cosine.T, portion[0], precision=lax.Precision.HIGHEST, preferred_element_type=jnp.float32
    )
    return first + jnp.dot(
        sine.T, portion[1], precision=lax.Precision.HIGHEST, preferred_element_type=jnp.float32
    )


LANES = 128
RADIX = 16
TILE = 8
MESH = pl.DeviceIdType.MESH


def level_weights(gaps):
    levels = gaps + 1
    summed = np.tril(np.ones((levels, gaps)), -1)
    deriv = np.zeros((levels, levels))
    for row in range(levels):
        if row < 4:
            deriv[row, :6] = BOUNDARY[row]
        elif row >= levels - 4:
            deriv[row, ::-1][:6] = -np.array(BOUNDARY[levels - 1 - row])
        else:
            deriv[row, row - 2 : row + 3] = np.array([1.0, -8.0, 0.0, 8.0, -1.0]) / 12.0
    return np.stack([summed, deriv @ summed]).astype(np.float32)


def transform_tables(modes, groups):
    part = NX // RADIX
    own = part // groups
    block = own + TILE
    rows = []
    for dest in range(groups):
        first = dest * own
        rows += list(range(first, first + own)) + [first - 1, first + own] + [first] * (TILE - 2)
    angle = 2.0 * np.pi / part * ((np.array(rows)[:, None] * np.arange(part)[None]) % part)
    full = np.concatenate([np.cos(angle), np.sin(angle)], axis=1).astype(np.float32)
    turn = 2.0 * np.pi / NX * (np.arange(RADIX)[:, None] * np.arange(part)[None])
    twiddle = np.concatenate([np.cos(turn), np.sin(turn)], axis=1).astype(np.float32)
    return full, twiddle, block


def rotate(value, angle):
    re, im = value
    cos, sin = math.cos(angle), math.sin(angle)
    if abs(sin) < 1e-12:
        return (re, im) if cos > 0 else (-re, -im)
    if abs(cos) < 1e-12:
        return (im, -re) if sin > 0 else (-im, re)
    if abs(abs(cos) - abs(sin)) < 1e-12:
        unit = math.sqrt(0.5)
        a, b = math.copysign(1.0, cos), math.copysign(1.0, sin)
        one = re * unit if a > 0 else re * -unit
        two = im * unit if a > 0 else im * -unit
        if a == b:
            return one + two, two - one
        return one - two, two + one
    return re * cos + im * sin, im * cos - re * sin


def fourier(values):
    count = len(values)
    if count == 1:
        return values
    even, odd = fourier(values[0::2]), fourier(values[1::2])
    out = [None] * count
    for i in range(count // 2):
        re, im = rotate(odd[i], 2.0 * math.pi * i / count)
        out[i] = (even[i][0] + re, even[i][1] + im)
        out[i + count // 2] = (even[i][0] - re, even[i][1] - im)
    return out


def split(value):
    high = value.astype(jnp.bfloat16)
    return high, (value - high.astype(jnp.float32)).astype(jnp.bfloat16)


def regroup(values, lane, width):
    values = list(values)
    step = len(values) // 2
    while step:
        upper = (lane // width) & step != 0
        shift = step * width
        for i in range(len(values)):
            if not i & step:
                low, high = values[i], values[i + step]
                values[i] = jnp.where(upper, pltpu.roll(high, shift, 1), low)
                values[i + step] = jnp.where(upper, high, pltpu.roll(low, LANES - shift, 1))
        step //= 2
    return values


def surface_kernel(
    groups, columns, coef, spacing, weights, basis_high_hbm, basis_low_hbm, twiddle,
    s_out, dx_out, dy_out, table,
    basis_high, basis_low, turned, gathered, high, low, product, landed, above, below,
    extended_s, outer, best, bests,
    const_sem, send_one, recv_one, send_two, recv_two, send_side, recv_side, send_max, recv_max,
):
    gx, gy = lax.axis_index("gx"), lax.axis_index("gy")
    loads = [
        pltpu.make_async_copy(basis_high_hbm, basis_high, const_sem.at[0]),
        pltpu.make_async_copy(basis_low_hbm, basis_low, const_sem.at[1]),
    ]
    for load in loads:
        load.start()
    barrier = pltpu.get_barrier_semaphore()
    for d in range(1, groups):
        pl.semaphore_signal(
            barrier, inc=1, device_id=(lax.rem(gx + d, groups), gy), device_id_type=MESH
        )
    for d in range(1, columns):
        pl.semaphore_signal(
            barrier, inc=1, device_id=(gx, lax.rem(gy + d, columns)), device_id_type=MESH
        )

    part = coef.shape[1]
    ys = coef.shape[2] // groups
    turned[:, :part] = coef[0].T
    turned[:, part:] = coef[1].T
    pl.semaphore_wait(barrier, groups + columns - 2)

    first = []
    for d in range(1, groups):
        target = lax.rem(gx + d, groups)
        copy = pltpu.make_async_remote_copy(
            src_ref=turned.at[pl.ds(pl.multiple_of(target * ys, TILE), ys)],
            dst_ref=gathered.at[gx],
            send_sem=send_one.at[d],
            recv_sem=recv_one.at[d],
            device_id=(target, gy),
            device_id_type=MESH,
        )
        copy.start()
        first.append(copy)
    gathered[gx] = turned[pl.ds(pl.multiple_of(gx * ys, TILE), ys), :]

    thick = spacing[...]
    total = jnp.sum(thick, axis=1, keepdims=True)
    scale = spacing.shape[1] * 1.0
    levels = spacing.shape[1] + 1
    stretch = jnp.sum(weights[0] * thick, axis=1, keepdims=True) / total
    slope = jnp.sum(weights[1] * thick, axis=1, keepdims=True) / total
    least = jnp.min(slope, axis=0, keepdims=True)
    table[0] = jnp.broadcast_to(scale * stretch, (levels, LANES))
    table[1] = jnp.broadcast_to(scale * (1.0 - stretch), (levels, LANES))
    table[2] = jnp.broadcast_to(scale * slope, (levels, LANES))

    for copy in first:
        copy.wait()

    half = NX // RADIX
    parts = half // part
    values = []
    for i in range(RADIX // 2):
        re = [gathered[i * parts + p, :, :part] for p in range(parts)]
        im = [gathered[i * parts + p, :, part:] for p in range(parts)]
        values.append(
            (re[0], im[0]) if parts == 1 else (jnp.concatenate(re, 1), jnp.concatenate(im, 1))
        )
    even = fourier(values)
    odd = fourier([rotate(v, 2.0 * math.pi * i / RADIX) for i, v in enumerate(values)])
    for r in range(RADIX):
        re, im = (even if r % 2 == 0 else odd)[r // 2]
        if r:
            cos, sin = twiddle[r : r + 1, :half], twiddle[r : r + 1, half:]
            re, im = re * cos + im * sin, im * cos - re * sin
        rows = slice(r * ys, (r + 1) * ys)
        high[rows, :half], low[rows, :half] = split(re)
        high[rows, half:], low[rows, half:] = split(im)

    for load in loads:
        load.wait()
    dot = functools.partial(
        lax.dot_general,
        dimension_numbers=(((1,), (1,)), ((), ())),
        preferred_element_type=jnp.float32,
    )
    raw = dot(basis_high[...], high[...])
    raw = raw + dot(basis_high[...], low[...])
    raw = raw + dot(basis_low[...], high[...])
    product[...] = raw
    block = landed.shape[1]
    own = block - TILE
    top = jnp.max(raw, axis=0, keepdims=True)
    for dest in range(groups):
        product[dest * block + own + 2 : dest * block + own + 3, :] = top

    second = []
    for d in range(1, groups):
        target = lax.rem(gx + d, groups)
        copy = pltpu.make_async_remote_copy(
            src_ref=product.at[pl.ds(pl.multiple_of(target * block, TILE), block)],
            dst_ref=landed.at[gx],
            send_sem=send_two.at[d],
            recv_sem=recv_two.at[d],
            device_id=(target, gy),
            device_id_type=MESH,
        )
        copy.start()
        second.append(copy)
    landed[gx] = product[pl.ds(pl.multiple_of(gx * block, TILE), block), :]
    for copy in second:
        copy.wait()

    side = []
    for i, (source, dest, d) in enumerate(((0, above, columns - 1), (groups - 1, below, 1))):
        copy = pltpu.make_async_remote_copy(
            src_ref=landed.at[source],
            dst_ref=dest,
            send_sem=send_side.at[i],
            recv_sem=recv_side.at[i],
            device_id=(gx, lax.rem(gy + d, columns)),
            device_id_type=MESH,
        )
        copy.start()
        side.append(copy)
    top = landed[0, own + 2 : own + 3, :]
    for j in range(1, groups):
        top = jnp.maximum(top, landed[j, own + 2 : own + 3, :])
    best[...] = jnp.broadcast_to(jnp.max(top, axis=1, keepdims=True), (TILE, LANES))
    maxima = []
    for d in range(1, columns):
        copy = pltpu.make_async_remote_copy(
            src_ref=best,
            dst_ref=bests.at[d],
            send_sem=send_max.at[d],
            recv_sem=recv_max.at[d],
            device_id=(gx, lax.rem(gy + d, columns)),
            device_id_type=MESH,
        )
        copy.start()
        maxima.append(copy)

    count = own * RADIX
    lane = lax.broadcasted_iota(jnp.int32, (block, LANES), 1)
    fold = LANES // ys
    for part_id in range(RADIX // fold):
        lanes = slice(part_id * LANES, (part_id + 1) * LANES)
        pieces = regroup([landed[j, :, lanes] for j in range(groups)], lane, ys)
        for i, piece in enumerate(pieces):
            r = part_id * fold + i
            piece = TOPO_SCALE * jnp.tanh(piece * 0.25)
            extended_s[pl.ds(TILE + r, own, stride=RADIX), :] = piece[:own]
            if r >= RADIX - 2:
                at = TILE - RADIX + r
                extended_s[at : at + 1, :] = piece[own : own + 1]
            if r < 2:
                at = TILE + count + r
                extended_s[at : at + 1, :] = piece[own + 1 : own + 2]
    s_out[...] = extended_s[TILE : TILE + count, :]
    dx_out[...] = (
        8.0 * (extended_s[TILE + 1 : TILE + 1 + count, :] - extended_s[TILE - 1 : TILE - 1 + count, :])
        - (extended_s[TILE + 2 : TILE + 2 + count, :] - extended_s[TILE - 2 : TILE - 2 + count, :])
    ) * (1.0 / 12.0)

    for copy in side:
        copy.wait()
    lane = lax.broadcasted_iota(jnp.int32, (own, LANES), 1)
    for r in range(RADIX):
        lanes = slice(r // fold * LANES, (r // fold + 1) * LANES)
        at = r % fold
        right, left = above[:own, lanes], below[:own, lanes]
        if at:
            right = pltpu.roll(right, LANES - at * ys, 1)
        if at != fold - 1:
            left = pltpu.roll(left, (fold - 1 - at) * ys, 1)
        piece = jnp.where(lane < LANES // 2, right, left)
        outer[pl.ds(r, own, stride=RADIX), :] = TOPO_SCALE * jnp.tanh(piece * 0.25)
    inner, edge = s_out[...], outer[...]
    lane = lax.broadcasted_iota(jnp.int32, (count, LANES), 1)

    def moved(by):
        taken = lane < by if by > 0 else lane >= LANES + by
        return pltpu.roll(jnp.where(taken, edge, inner), (LANES - by) % LANES, 1)

    dy_out[...] = (8.0 * (moved(1) - moved(-1)) - (moved(2) - moved(-2))) * (1.0 / 12.0)

    for copy in maxima:
        copy.wait()
    peak = best[0:1, :]
    for d in range(1, columns):
        peak = jnp.maximum(peak, bests[d, 0:1, :])
    peak = TOPO_SCALE * jnp.tanh(peak * 0.25)
    table[3] = jnp.broadcast_to(slope, (levels, LANES)) / ((1.0 - peak) * least)


def surface_by_kernel(coefficients, spacing, groups, columns):
    _, modes, ys = coefficients.shape
    full, twiddle, block = transform_tables(modes * groups, groups)
    high = full.astype(jnp.bfloat16)
    low = (full - high.astype(np.float32)).astype(jnp.bfloat16)
    weights = level_weights(spacing.shape[0])
    levels = spacing.shape[0] + 1
    count = NX // groups
    part = NX // RADIX
    width = RADIX * (ys // groups)
    vmem = pl.BlockSpec(memory_space=pltpu.VMEM)
    hbm = pl.BlockSpec(memory_space=pl.ANY)
    plane = jax.ShapeDtypeStruct((count, ys), jnp.float32)
    dma = pltpu.SemaphoreType.DMA
    return pl.pallas_call(
        functools.partial(surface_kernel, groups, columns),
        out_shape=(plane, plane, plane, jax.ShapeDtypeStruct((4, levels, LANES), jnp.float32)),
        in_specs=[vmem, vmem, vmem, hbm, hbm, vmem],
        out_specs=(vmem,) * 4,
        scratch_shapes=[
            pltpu.VMEM(full.shape, jnp.bfloat16),
            pltpu.VMEM(full.shape, jnp.bfloat16),
            pltpu.VMEM((ys, 2 * modes), jnp.float32),
            pltpu.VMEM((groups, ys // groups, 2 * modes), jnp.float32),
            pltpu.VMEM((width, 2 * part), jnp.bfloat16),
            pltpu.VMEM((width, 2 * part), jnp.bfloat16),
            pltpu.VMEM((groups * block, width), jnp.float32),
            pltpu.VMEM((groups, block, width), jnp.float32),
            pltpu.VMEM((block, width), jnp.float32),
            pltpu.VMEM((block, width), jnp.float32),
            pltpu.VMEM((count + 2 * TILE, ys), jnp.float32),
            pltpu.VMEM((count, ys), jnp.float32),
            pltpu.VMEM((TILE, LANES), jnp.float32),
            pltpu.VMEM((columns, TILE, LANES), jnp.float32),
            dma((2,)),
            dma((groups,)),
            dma((groups,)),
            dma((groups,)),
            dma((groups,)),
            dma((2,)),
            dma((2,)),
            dma((columns,)),
            dma((columns,)),
        ],
        compiler_params=pltpu.CompilerParams(collective_id=0, has_side_effects=True),
    )(coefficients, spacing[None], jnp.asarray(weights), jnp.asarray(high), jnp.asarray(low), jnp.asarray(twiddle))


def surface_by_gather(coefficients, spacing, groups):
    x_count = NX // groups
    x_first = lax.axis_index("gx") * x_count
    x_cells = x_first + jnp.arange(x_count, dtype=jnp.int32)
    portion = lax.all_gather(coefficients, "gx", axis=1, tiled=True)
    cosine, sine = basis(portion.shape[1], x_cells)
    surface = TOPO_SCALE * jnp.tanh(project(cosine, sine, portion) * 0.25)
    stretch = stretching(spacing)
    scale = stretch.shape[0] - 1.0
    slope = vertical(stretch)
    peak = lax.pmax(jnp.max(surface), ("gx", "gy"))
    wide = extended(surface, (("gx", 0), ("gy", 1)), 2)
    dx = (8.0 * (wide[3:-1] - wide[1:-3]) - (wide[4:] - wide[:-4]))[:, 2:-2] / 12.0
    dy = (8.0 * (wide[:, 3:-1] - wide[:, 1:-3]) - (wide[:, 4:] - wide[:, :-4]))[2:-2] / 12.0
    rows = [scale * stretch, scale * (1.0 - stretch), scale * slope]
    rows.append(slope / ((1.0 - peak) * jnp.min(slope)))
    table = jnp.broadcast_to(jnp.stack(rows)[:, :, None], (4, stretch.shape[0], LANES))
    return surface, dx, dy, table


def levels_kernel(depth, s_ref, dx_ref, dy_ref, table, z_ref, slopes_ref, jac_ref, quality_ref):
    first = pl.program_id(0) * depth

    def row(which, level):
        return table[which, pl.ds(first + level, 1), :]

    for level in range(depth):
        s, gain = s_ref[...], row(1, level)
        z_ref[level] = row(0, level) + gain * s
        slopes_ref[0, level] = gain * dx_ref[...]
        slopes_ref[1, level] = gain * dy_ref[...]
        rest = 1.0 - s
        jac_ref[level] = row(2, level) * rest
        quality_ref[level] = row(3, level) * rest


def all_levels(s, dx, dy, table):
    levels = table.shape[1]
    rows, columns = s.shape
    depth = 2
    plane = pl.BlockSpec((rows, columns), lambda i: (0, 0))
    field = pl.BlockSpec((depth, rows, columns), lambda i: (i, 0, 0))
    shape = jax.ShapeDtypeStruct((levels, rows, columns), jnp.float32)
    return pl.pallas_call(
        functools.partial(levels_kernel, depth),
        grid=(levels // depth,),
        in_specs=[plane, plane, plane, pl.BlockSpec(table.shape, lambda i: (0, 0, 0))],
        out_specs=(
            field,
            pl.BlockSpec((2, depth, rows, columns), lambda i: (0, i, 0, 0)),
            field,
            field,
        ),
        out_shape=(
            shape,
            jax.ShapeDtypeStruct((2, levels, rows, columns), jnp.float32),
            shape,
            shape,
        ),
    )(s, dx, dy, table)


def shards(coefficients, spacing):
    groups, columns = lax.axis_size("gx"), lax.axis_size("gy")
    _, modes, ys = coefficients.shape
    fits = (
        ys == LANES
        and modes % LANES == 0
        and modes * groups * 2 == NX
        and ys % (groups * RADIX) == 0
        and groups * (ys // groups) == LANES
        and (NX // RADIX) % (groups * TILE) == 0
        and columns > 1
    )
    if fits:
        parts = surface_by_kernel(coefficients, spacing, groups, columns)
    else:
        parts = surface_by_gather(coefficients, spacing, groups)
    return all_levels(*parts)


def solution(mesh):
    return jax.shard_map(
        shards,
        mesh=mesh,
        in_specs=(P(None, "gx", "gy"), P()),
        out_specs=(
            P(None, "gx", "gy"),
            P(None, None, "gx", "gy"),
            P(None, "gx", "gy"),
            P(None, "gx", "gy"),
        ),
        check_vma=False,
    )
```

profile of v0, /device:TPU:0, one launch (start us, length us, event | category | flops | bytes accessed | tf_op | source)
XLA Modules:
  0.0 38.9 jit_solution(7585478742446160322)
XLA Ops:
  0.6 23.7 %shard_map.93 = (f32[512,128]{1,0:T(8,128)}, f32[512,128]{1,0:T(8,128)}, f32[512,128]{1,0:T(8,128)}, f32[4,32,128]{2,1,0:T(8,128)}) custom-call(f32[2,256,128]{2,1,0:T(8,128)} %coef.1, f32[1,31]{1,0:T(1,128)} %bitcast.1, f32[2,32,31]{2,1,0:T(8,128)} %constant.8.clone.weights, bf16[320,512]{1,0:T(8,128)(2,1)} %constant.9.clone.basis_high_hbm, ...), custom_call_target="tpu_custom_call" | custom-call | tf_op jit(solution)/shard_map/pallas_call | solution.py:382
  24.4 14.6 %shard_map.94 = (f32[32,512,128]{2,1,0:T(8,128)}, f32[2,32,512,128]{3,2,1,0:T(8,128)}, f32[32,512,128]{2,1,0:T(8,128)}, f32[32,512,128]{2,1,0:T(8,128)}) custom-call(f32[512,128]{1,0:T(8,128)} %get-tuple-element.8.s_ref, f32[512,128]{1,0:T(8,128)} %get-tuple-element.9.dx_ref, f32[512,128]{1,0:T(8,128)} %get-tuple-element.10.dy_ref, ...), custom_call_target="tpu_custom_call" | custom-call | tf_op jit(solution)/shard_map/pallas_call | solution.py:459
where the time goes:
time: 39.1 us; the launch traced here: 38.9 us
  Pallas kernels  38.3 us (98%)
  between operations  0.64 us (2%)
    pallas_call x1, Pallas kernels, surface_by_kernel(): pl.pallas_call(functools.partial(surface_kernel, groups, columns), out_sh...  23.7 us
    pallas_call x1, Pallas kernels, all_levels(): pl.pallas_call(functools.partial(levels_kernel, depth), grid=(levels // d...  14.6 us

commit v1 on v0

--- a/solution.py
+++ b/solution.py
@@ -174,10 +174,14 @@
     groups, columns, coef, spacing, weights, basis_high_hbm, basis_low_hbm, twiddle,
     s_out, dx_out, dy_out, table,
     basis_high, basis_low, turned, gathered, high, low, product, landed, above, below,
-    extended_s, outer, best, bests,
+    extended_s, outer, best, bests, edges, edge_product,
     const_sem, send_one, recv_one, send_two, recv_two, send_side, recv_side, send_max, recv_max,
 ):
     gx, gy = lax.axis_index("gx"), lax.axis_index("gy")
+
+    def moved_by(d):
+        return lax.rem(gx + d // columns, groups), lax.rem(gy + d % columns, columns)
+
     loads = [
         pltpu.make_async_copy(basis_high_hbm, basis_high, const_sem.at[0]),
         pltpu.make_async_copy(basis_low_hbm, basis_low, const_sem.at[1]),
@@ -185,20 +189,14 @@
     for load in loads:
         load.start()
     barrier = pltpu.get_barrier_semaphore()
-    for d in range(1, groups):
-        pl.semaphore_signal(
-            barrier, inc=1, device_id=(lax.rem(gx + d, groups), gy), device_id_type=MESH
-        )
-    for d in range(1, columns):
-        pl.semaphore_signal(
-            barrier, inc=1, device_id=(gx, lax.rem(gy + d, columns)), device_id_type=MESH
-        )
+    for d in range(1, groups * columns):
+        pl.semaphore_signal(barrier, inc=1, device_id=moved_by(d), device_id_type=MESH)
 
     part = coef.shape[1]
     ys = coef.shape[2] // groups
     turned[:, :part] = coef[0].T
     turned[:, part:] = coef[1].T
-    pl.semaphore_wait(barrier, groups + columns - 2)
+    pl.semaphore_wait(barrier, groups * columns - 1)
 
     first = []
     for d in range(1, groups):
@@ -248,6 +246,9 @@
         rows = slice(r * ys, (r + 1) * ys)
         high[rows, :half], low[rows, :half] = split(re)
         high[rows, half:], low[rows, half:] = split(im)
+        rows = slice(r * TILE, (r + 1) * TILE)
+        edges[rows, :half] = jnp.where(gx == 0, re[:TILE], re[ys - TILE :])
+        edges[rows, half:] = jnp.where(gx == 0, im[:TILE], im[ys - TILE :])
 
     for load in loads:
         load.wait()
@@ -259,18 +260,33 @@
     raw = dot(basis_high[...], high[...])
     raw = raw + dot(basis_high[...], low[...])
     raw = raw + dot(basis_low[...], high[...])
-    product[...] = raw
-    block = landed.shape[1]
+    best[...] = jnp.broadcast_to(jnp.max(raw, keepdims=True), (TILE, LANES))
+    maxima = []
+    for d in range(1, groups * columns):
+        copy = pltpu.make_async_remote_copy(
+            src_ref=best,
+            dst_ref=bests.at[d],
+            send_sem=send_max.at[d],
+            recv_sem=recv_max.at[d],
+            device_id=moved_by(d),
+            device_id_type=MESH,
+        )
+        copy.start()
+        maxima.append(copy)
+    block = basis_high.shape[0] // groups
     own = block - TILE
-    top = jnp.max(raw, axis=0, keepdims=True)
+    sublane = lax.broadcasted_iota(jnp.int32, (TILE, LANES), 0)
     for dest in range(groups):
-        product[dest * block + own + 2 : dest * block + own + 3, :] = top
+        rows = raw[dest * block : (dest + 1) * block]
+        product[dest, :own] = rows[:own, :LANES]
+        product[dest, own : 2 * own] = rows[:own, LANES:]
+        product[dest, 2 * own :] = jnp.where(sublane == 0, rows[own:, LANES:], rows[own:, :LANES])
 
     second = []
     for d in range(1, groups):
         target = lax.rem(gx + d, groups)
         copy = pltpu.make_async_remote_copy(
-            src_ref=product.at[pl.ds(pl.multiple_of(target * block, TILE), block)],
+            src_ref=product.at[target],
             dst_ref=landed.at[gx],
             send_sem=send_two.at[d],
             recv_sem=recv_two.at[d],
@@ -279,74 +295,71 @@
         )
         copy.start()
         second.append(copy)
-    landed[gx] = product[pl.ds(pl.multiple_of(gx * block, TILE), block), :]
+    landed[gx] = product[gx]
+
+    edge_high, edge_low = split(edges[...])
+    raw = dot(basis_high[...], edge_high)
+    raw = raw + dot(basis_high[...], edge_low)
+    raw = raw + dot(basis_low[...], edge_high)
+    for dest in range(groups):
+        edge_product[dest] = raw[dest * block : dest * block + own]
+
+    def side_copy(which, dest):
+        return pltpu.make_async_remote_copy(
+            src_ref=edge_product.at[dest],
+            dst_ref=(above, below)[which],
+            send_sem=send_side.at[dest],
+            recv_sem=recv_side.at[which],
+            device_id=(dest, lax.rem(gy + (columns - 1, 1)[which], columns)),
+            device_id_type=MESH,
+        )
+
+    for which, sender in enumerate((0, groups - 1)):
+
+        @pl.when(gx == sender)
+        def _():
+            for dest in range(groups):
+                side_copy(which, dest).start()
+
     for copy in second:
         copy.wait()
 
-    side = []
-    for i, (source, dest, d) in enumerate(((0, above, columns - 1), (groups - 1, below, 1))):
-        copy = pltpu.make_async_remote_copy(
-            src_ref=landed.at[source],
-            dst_ref=dest,
-            send_sem=send_side.at[i],
-            recv_sem=recv_side.at[i],
-            device_id=(gx, lax.rem(gy + d, columns)),
-            device_id_type=MESH,
-        )
-        copy.start()
-        side.append(copy)
-    top = landed[0, own + 2 : own + 3, :]
-    for j in range(1, groups):
-        top = jnp.maximum(top, landed[j, own + 2 : own + 3, :])
-    best[...] = jnp.broadcast_to(jnp.max(top, axis=1, keepdims=True), (TILE, LANES))
-    maxima = []
-    for d in range(1, columns):
-        copy = pltpu.make_async_remote_copy(
-            src_ref=best,
-            dst_ref=bests.at[d],
-            send_sem=send_max.at[d],
-            recv_sem=recv_max.at[d],
-            device_id=(gx, lax.rem(gy + d, columns)),
-            device_id_type=MESH,
-        )
-        copy.start()
-        maxima.append(copy)
-
     count = own * RADIX
-    lane = lax.broadcasted_iota(jnp.int32, (block, LANES), 1)
-    fold = LANES // ys
-    for part_id in range(RADIX // fold):
-        lanes = slice(part_id * LANES, (part_id + 1) * LANES)
-        pieces = regroup([landed[j, :, lanes] for j in range(groups)], lane, ys)
+    lane = lax.broadcasted_iota(jnp.int32, (own, LANES), 1)
+    for part_id in range(RADIX // groups):
+        rows = slice(part_id * own, (part_id + 1) * own)
+        pieces = regroup([landed[j, rows, :] for j in range(groups)], lane, ys)
         for i, piece in enumerate(pieces):
-            r = part_id * fold + i
-            piece = TOPO_SCALE * jnp.tanh(piece * 0.25)
-            extended_s[pl.ds(TILE + r, own, stride=RADIX), :] = piece[:own]
-            if r >= RADIX - 2:
-                at = TILE - RADIX + r
-                extended_s[at : at + 1, :] = piece[own : own + 1]
-            if r < 2:
-                at = TILE + count + r
-                extended_s[at : at + 1, :] = piece[own + 1 : own + 2]
+            r = part_id * groups + i
+            extended_s[pl.ds(TILE + r, own, stride=RADIX), :] = TOPO_SCALE * jnp.tanh(piece * 0.25)
+    lane = lax.broadcasted_iota(jnp.int32, (TILE, LANES), 1)
+    pieces = regroup([landed[j, 2 * own :, :] for j in range(groups)], lane, ys)
+    for i in range(2):
+        before = TOPO_SCALE * jnp.tanh(pieces[groups - 2 + i] * 0.25)
+        after = TOPO_SCALE * jnp.tanh(pieces[i] * 0.25)
+        extended_s[TILE - 2 + i : TILE - 1 + i, :] = before[0:1]
+        extended_s[TILE + count + i : TILE + count + i + 1, :] = after[1:2]
     s_out[...] = extended_s[TILE : TILE + count, :]
     dx_out[...] = (
         8.0 * (extended_s[TILE + 1 : TILE + 1 + count, :] - extended_s[TILE - 1 : TILE - 1 + count, :])
         - (extended_s[TILE + 2 : TILE + 2 + count, :] - extended_s[TILE - 2 : TILE - 2 + count, :])
     ) * (1.0 / 12.0)
 
-    for copy in side:
-        copy.wait()
+    for which, sender in enumerate((0, groups - 1)):
+        side_copy(which, 0).wait_recv()
+
+        @pl.when(gx == sender)
+        def _():
+            for dest in range(groups):
+                side_copy(which, dest).wait_send()
+
     lane = lax.broadcasted_iota(jnp.int32, (own, LANES), 1)
+    right_all = TOPO_SCALE * jnp.tanh(above[...] * 0.25)
+    left_all = TOPO_SCALE * jnp.tanh(below[...] * 0.25)
     for r in range(RADIX):
-        lanes = slice(r // fold * LANES, (r // fold + 1) * LANES)
-        at = r % fold
-        right, left = above[:own, lanes], below[:own, lanes]
-        if at:
-            right = pltpu.roll(right, LANES - at * ys, 1)
-        if at != fold - 1:
-            left = pltpu.roll(left, (fold - 1 - at) * ys, 1)
-        piece = jnp.where(lane < LANES // 2, right, left)
-        outer[pl.ds(r, own, stride=RADIX), :] = TOPO_SCALE * jnp.tanh(piece * 0.25)
+        right = pltpu.roll(right_all, LANES - r * TILE, 1) if r else right_all
+        left = pltpu.roll(left_all, LANES - TILE - r * TILE, 1) if r != RADIX - 1 else left_all
+        outer[pl.ds(r, own, stride=RADIX), :] = jnp.where(lane < LANES // 2, right, left)
     inner, edge = s_out[...], outer[...]
     lane = lax.broadcasted_iota(jnp.int32, (count, LANES), 1)
 
@@ -359,7 +372,7 @@
     for copy in maxima:
         copy.wait()
     peak = best[0:1, :]
-    for d in range(1, columns):
+    for d in range(1, groups * columns):
         peak = jnp.maximum(peak, bests[d, 0:1, :])
     peak = TOPO_SCALE * jnp.tanh(peak * 0.25)
     table[3] = jnp.broadcast_to(slope, (levels, LANES)) / ((1.0 - peak) * least)
@@ -375,6 +388,7 @@
     count = NX // groups
     part = NX // RADIX
     width = RADIX * (ys // groups)
+    own = block - TILE
     vmem = pl.BlockSpec(memory_space=pltpu.VMEM)
     hbm = pl.BlockSpec(memory_space=pl.ANY)
     plane = jax.ShapeDtypeStruct((count, ys), jnp.float32)
@@ -391,23 +405,25 @@
             pltpu.VMEM((groups, ys // groups, 2 * modes), jnp.float32),
             pltpu.VMEM((width, 2 * part), jnp.bfloat16),
             pltpu.VMEM((width, 2 * part), jnp.bfloat16),
-            pltpu.VMEM((groups * block, width), jnp.float32),
-            pltpu.VMEM((groups, block, width), jnp.float32),
-            pltpu.VMEM((block, width), jnp.float32),
-            pltpu.VMEM((block, width), jnp.float32),
+            pltpu.VMEM((groups, 2 * own + TILE, LANES), jnp.float32),
+            pltpu.VMEM((groups, 2 * own + TILE, LANES), jnp.float32),
+            pltpu.VMEM((own, LANES), jnp.float32),
+            pltpu.VMEM((own, LANES), jnp.float32),
             pltpu.VMEM((count + 2 * TILE, ys), jnp.float32),
             pltpu.VMEM((count, ys), jnp.float32),
             pltpu.VMEM((TILE, LANES), jnp.float32),
-            pltpu.VMEM((columns, TILE, LANES), jnp.float32),
+            pltpu.VMEM((groups * columns, TILE, LANES), jnp.float32),
+            pltpu.VMEM((RADIX * TILE, 2 * part), jnp.float32),
+            pltpu.VMEM((groups, own, LANES), jnp.float32),
             dma((2,)),
             dma((groups,)),
             dma((groups,)),
             dma((groups,)),
             dma((groups,)),
+            dma((groups,)),
             dma((2,)),
-            dma((2,)),
-            dma((columns,)),
-            dma((columns,)),
+            dma((groups * columns,)),
+            dma((groups * columns,)),
         ],
         compiler_params=pltpu.CompilerParams(collective_id=0, has_side_effects=True),
     )(coefficients, spacing[None], jnp.asarray(weights), jnp.asarray(high), jnp.asarray(low), jnp.asarray(twiddle))
@@ -483,7 +499,8 @@
         and modes % LANES == 0
         and modes * groups * 2 == NX
         and ys % (groups * RADIX) == 0
-        and groups * (ys // groups) == LANES
+        and ys == groups * RADIX
+        and groups * TILE * 2 == RADIX * TILE
         and (NX // RADIX) % (groups * TILE) == 0
         and columns > 1
     )

time: 39.1 us -> 38.4 us (0.982)
  Pallas kernels: 38.3 us -> 37.5 us
    pallas_call x1, Pallas kernels: 23.7 us -> 22.9 us  [surface_by_kernel(): pl.pallas_call(functools.partial(surface_kernel, groups, columns), out_sh...]
where the time goes in v1:
time: 38.4 us; the launch traced here: 38.1 us
  Pallas kernels  37.5 us (98%)
  between operations  0.64 us (2%)
    pallas_call x1, Pallas kernels, surface_by_kernel(): pl.pallas_call(functools.partial(surface_kernel, groups, columns), out_sh...  22.9 us
    pallas_call x1, Pallas kernels, all_levels(): pl.pallas_call(functools.partial(levels_kernel, depth), grid=(levels // d...  14.6 us

profile of v1, /device:TPU:0, one launch (start us, length us, event | category | flops | bytes accessed | tf_op | source)
XLA Modules:
  0.0 38.1 jit_solution(14844222767014426257)
XLA Ops:
  0.6 22.9 %shard_map.93 = (f32[512,128]{1,0:T(8,128)}, f32[512,128]{1,0:T(8,128)}, f32[512,128]{1,0:T(8,128)}, f32[4,32,128]{2,1,0:T(8,128)}) custom-call(f32[2,256,128]{2,1,0:T(8,128)} %coef.1, f32[1,31]{1,0:T(1,128)} %bitcast.1, f32[2,32,31]{2,1,0:T(8,128)} %constant.8.clone.weights, bf16[320,512]{1,0:T(8,128)(2,1)} %constant.9.clone.basis_high_hbm, ...), custom_call_target="tpu_custom_call" | custom-call | tf_op jit(solution)/shard_map/pallas_call | solution.py:396
  23.5 14.6 %shard_map.94 = (f32[32,512,128]{2,1,0:T(8,128)}, f32[2,32,512,128]{3,2,1,0:T(8,128)}, f32[32,512,128]{2,1,0:T(8,128)}, f32[32,512,128]{2,1,0:T(8,128)}) custom-call(f32[512,128]{1,0:T(8,128)} %get-tuple-element.8.s_ref, f32[512,128]{1,0:T(8,128)} %get-tuple-element.9.dx_ref, f32[512,128]{1,0:T(8,128)} %get-tuple-element.10.dy_ref, ...), custom_call_target="tpu_custom_call" | custom-call | tf_op jit(solution)/shard_map/pallas_call | solution.py:475
